TPU v7x, 32 devices: a whole 2x2x4 slice. The times are simulated.
32 devices in a mesh: member: 4 (over z), lat: 4 (over y, core), lon: 2 (over x).
Axes of the slice: x: 2, y: 2, z: 4, core: 2. Of those that a mesh axis runs over, the one named last changes fastest.
Arguments:
- state: bfloat16 [100, 8, 720], P(None, 'lat', 'lon'), may hold values from -6 to 6
- target: bfloat16 [100, 8, 720], P(None, 'lat', 'lon'), may hold values from -6 to 6
- land_sea: int32 [8, 720], P('lat', 'lon'), may hold values 0 or 1
- seeds: int32 [4, 32], P('member'), may hold values from 0 to 65535
- w_in: bfloat16 [9, 100, 256], replicated, may hold values from -0.1875 to 0.1875
- w_mid: bfloat16 [9, 256, 256], replicated, may hold values from -0.125 to 0.125
- w_out: bfloat16 [100, 256], replicated, may hold values from -0.375 to 0.375
- w_noise: float32 [32, 256], replicated, may hold values from -1 to 1
Outputs:
- update_in: float32 [9, 100, 256], replicated
- update_mid: float32 [9, 256, 256], replicated
- update_out: float32 [100, 256], replicated
- update_noise: float32 [32, 256], replicated
- loss: float32 [], replicated
All inputs are finite; a program needn't handle non-finite values. No bound on the sum of `land_sea` on one device may be relied on, other than what follows from the above.
Results may differ from a plain program's by a relative error of at most 0.0014.
Values may be sent and summed in bfloat16 or wider, within the bound.
A program may use at most 64 MiB of HBM per device.

v0:
```python
import jax
import jax.numpy as jnp
from jax import lax
from jax.sharding import PartitionSpec as P

SMOOTH = 0.25


def with_halo(block, sides, width):
    for axis, dim in sides:
        count = lax.axis_size(axis)
        forward = [(i, i + 1) for i in range(count - 1)]
        forward.append((count - 1, 0))
        backward = [(target, source) for source, target in forward]
        low = lax.ppermute(
            lax.slice_in_dim(block, block.shape[dim] - width, None, axis=dim), axis, forward
        )
        high = lax.ppermute(lax.slice_in_dim(block, 0, width, axis=dim), axis, backward)
        block = jnp.concatenate([low, block, high], axis=dim)
    return block


def shifted(padded, offset, row_count, col_count):
    row_shift = offset // 3
    col_shift = offset % 3
    window = padded[:, row_shift : row_shift + row_count, col_shift : col_shift + col_count]
    return window.reshape(padded.shape[0], row_count * col_count)


def conv_forward(weights, padded, row_count, col_count):
    summed = None
    for offset in range(9):
        window = shifted(padded, offset, row_count, col_count)
        part = lax.dot_general(
            weights[offset], window, (((0,), (0,)), ((), ())), preferred_element_type=jnp.float32
        )
        summed = part if summed is None else summed + part
    return summed


def conv_back(weights, padded, row_count, col_count):
    summed = None
    for offset in range(9):
        window = shifted(padded, 8 - offset, row_count, col_count)
        part = jnp.dot(weights[offset], window, preferred_element_type=jnp.float32)
        summed = part if summed is None else summed + part
    return summed


def weight_grad(padded, deltas, row_count, col_count):
    parts = []
    for offset in range(9):
        window = shifted(padded, offset, row_count, col_count)
        parts.append(
            lax.dot_general(
                window, deltas, (((1,), (1,)), ((), ())), preferred_element_type=jnp.float32
            )
        )
    return jnp.stack(parts)


def gelu_pair(pre):
    return jax.jvp(jax.nn.gelu, (pre,), (jnp.ones_like(pre),))


def clear_outside(padded, width, lat_index, lat_count):
    row_count = padded.shape[1] - 2 * width
    global_row = lat_index * row_count + jnp.arange(padded.shape[1], dtype=jnp.int32) - width
    inside = (global_row >= 0) & (global_row < row_count * lat_count)
    return jnp.where(inside[None, :, None], padded, jnp.zeros((), padded.dtype))


def combine(outputs, target_flat, weights, slope_sum, spread_sum, members):
    misses = outputs - target_flat[None]
    radius = jnp.sqrt(misses * misses + SMOOTH * SMOOTH)
    gradients = weights[None] * (misses / radius / members - slope_sum / (members * (members - 1)))
    loss_term = jnp.sum(
        weights[None] * ((radius - SMOOTH) / members - spread_sum / (2 * members * (members - 1)))
    )
    return (gradients, loss_term)


def pair_sums(outputs, others, running):

    def add_member(totals, member_out):
        gap_value = outputs - member_out.astype(jnp.float32)[None]
        radius = jnp.sqrt(gap_value * gap_value + SMOOTH * SMOOTH)
        return ((totals[0] + gap_value / radius, totals[1] + radius - SMOOTH), None)

    sums, _ = lax.scan(add_member, running, others)
    return sums


def normalize(gradient):
    return gradient / jnp.sqrt(jnp.mean(gradient * gradient) + 1e-06)


def body(state, target, land_sea, seeds, w_in, w_mid, w_out, w_noise):
    variables, row_count, col_count = state.shape
    channels = w_in.shape[2]
    cell_count = row_count * col_count
    lat_index = lax.axis_index("lat")
    lat_count = lax.axis_size("lat")
    members = lax.axis_size("member")
    latent = (seeds[0].astype(jnp.float32) - 32767.5) / 18918.0
    noise_bias = jnp.dot(latent, w_noise, precision=lax.Precision.HIGHEST)
    state_pad = with_halo(state, (("lat", 1), ("lon", 2)), 1)
    state_pad = clear_outside(state_pad, 1, lat_index, lat_count)
    pre_in = conv_forward(w_in, state_pad, row_count, col_count) + noise_bias[:, None]
    act_in, slope_in = gelu_pair(pre_in)
    hidden_in = act_in.astype(jnp.bfloat16)
    hidden_pad = with_halo(
        hidden_in.reshape(channels, row_count, col_count), (("lat", 1), ("lon", 2)), 1
    )
    hidden_pad = clear_outside(hidden_pad, 1, lat_index, lat_count)
    pre_mid = conv_forward(w_mid, hidden_pad, row_count, col_count)
    act_mid, slope_mid = gelu_pair(pre_mid)
    hidden_out = (act_mid + hidden_in.astype(jnp.float32)).astype(jnp.bfloat16)
    flat_state = state.reshape(variables, cell_count).astype(jnp.float32)
    output = (flat_state + jnp.dot(w_out, hidden_out, preferred_element_type=jnp.float32)).astype(
        jnp.bfloat16
    )
    target_flat = target.reshape(variables, cell_count).astype(jnp.float32)
    weights = 1.0 + land_sea.reshape(1, cell_count).astype(jnp.float32)
    own_output = output.astype(jnp.float32)[None]
    blank = jnp.zeros(own_output.shape, jnp.float32)
    slope_sum, spread_sum = pair_sums(
        own_output, lax.all_gather(output[None], "member", axis=0, tiled=True), (blank, blank)
    )
    gradients, loss_term = combine(own_output, target_flat, weights, slope_sum, spread_sum, members)
    delta_out = gradients[0].astype(jnp.bfloat16)
    grad_out = lax.dot_general(
        delta_out, hidden_out, (((1,), (1,)), ((), ())), preferred_element_type=jnp.float32
    )
    upstream = lax.dot_general(
        w_out, delta_out, (((0,), (0,)), ((), ())), preferred_element_type=jnp.float32
    )
    delta_mid = (upstream * slope_mid).astype(jnp.bfloat16)
    delta_pad = with_halo(
        delta_mid.reshape(channels, row_count, col_count), (("lat", 1), ("lon", 2)), 1
    )
    delta_pad = clear_outside(delta_pad, 1, lat_index, lat_count)
    incoming = conv_back(w_mid, delta_pad, row_count, col_count) + upstream
    delta_in = (incoming * slope_in).astype(jnp.bfloat16)
    grad_mid = weight_grad(hidden_pad, delta_mid, row_count, col_count)
    grad_in = weight_grad(state_pad, delta_in, row_count, col_count)
    grad_noise = latent[:, None] * jnp.sum(delta_in.astype(jnp.float32), axis=1)[None, :]
    grad_in, grad_mid, grad_out, grad_noise, summed = lax.psum(
        (grad_in, grad_mid, grad_out, grad_noise, loss_term), ("member", "lat", "lon")
    )
    loss = summed / (variables * cell_count * lat_count * lax.axis_size("lon"))
    return (
        normalize(grad_in),
        normalize(grad_mid),
        normalize(grad_out),
        normalize(grad_noise),
        loss,
    )


def solution(mesh):
    placed = (
        P(None, "lat", "lon"),
        P(None, "lat", "lon"),
        P("lat", "lon"),
        P("member", None),
        P(),
        P(),
        P(),
        P(),
    )
    return jax.shard_map(
        body, mesh=mesh, in_specs=placed, out_specs=(P(), P(), P(), P(), P()), check_vma=False
    )
```

profile of v0, /device:TPU:0, one launch (start us, length us, event | category | flops | bytes accessed | tf_op | source)
XLA Modules:
  0.0 255.6 jit_solution(3920980561953618674)
XLA Ops:
  7.2 1.3 fusion.124
  8.5 2.5 collective-permute-start.1
  11.0 0.9 fusion.114
  11.9 3.4 %collective-permute-done.1 = bf16[100,1,360]{2,1,0:T(2,128)(2,1)S(1)} collective-permute-done((bf16[100,1,360]{2,1,0:T(2,128)(2,1)S(1)}, bf16[100,1,360]{2,1,0:T(2,128)(2,1)S(1)}, u32[]{:S(2)}, u32[]{:S(2)}) %collective-permute-start.1) | collective-permute-done | bytes 72032 | tf_op jit(solution)/shard_map/ppermute | solution.py:18
  15.3 1.1 collective-permute-done
  16.4 1.3 pad_maximum_fusion.2
  17.7 1.6 collective-permute-start.3
  19.2 0.5 collective-permute-start.2
  19.8 3.2 %collective-permute-done.3 = bf16[100,4,1]{2,1,0:T(4,128)(2,1)S(1)} collective-permute-done((bf16[100,4,1]{2,1,0:T(4,128)(2,1)S(1)}, bf16[100,4,1]{2,1,0:T(4,128)(2,1)S(1)}, u32[]{:S(2)}, u32[]{:S(2)}) %collective-permute-start.3) | collective-permute-done | bytes 832 | tf_op jit(solution)/shard_map/ppermute | solution.py:18
  23.0 1.1 collective-permute-done.2
  24.1 2.2 maximum_select_fusion.2
  26.3 1.4 fusion.123
  31.7 1.3 multiply_convert_fusion
  33.0 1.0 collective-permute-start.5
  34.1 4.3 %collective-permute-done.5 = bf16[256,1,360]{0,2,1:T(8,128)(2,1)S(1)} collective-permute-done((bf16[256,1,360]{0,2,1:T(8,128)(2,1)S(1)}, bf16[256,1,360]{0,2,1:T(8,128)(2,1)S(1)}, u32[]{:S(2)}, u32[]{:S(2)}) %collective-permute-start.5) | collective-permute-done | bytes 184352 | tf_op jit(solution)/shard_map/ppermute | solution.py:18
  38.4 2.3 collective-permute-done.4
  40.8 1.6 collective-permute-start.7
  42.3 0.5 collective-permute-start.6
  42.9 0.9 reshape.203
  43.8 0.8 reshape.204
  44.7 1.3 collective-permute-done.6
  46.8 0.8 copy-done.3
  49.8 1.3 add_convert_fusion
  51.4 16.8 %all-gather.1 = bf16[4,100,720]{2,1,0:T(8,128)(2,1)} all-gather(bf16[1,100,720]{2,1,0:T(8,128)(2,1)S(1)} %bitcast.306), channel_id=2, replica_groups=mesh['member'=4,'lat'=4,'lon'=2] {'member'}, dimensions={0}, use_global_device_ids=true | all-gather | bytes 720000 | tf_op jit(solution)/shard_map/all_gather | solution.py:128
  68.2 4.7 %while.15 = (s32[]{:T(128)}, f32[1,100,720]{2,1,0:T(8,128)S(1)}, f32[1,100,720]{2,1,0:T(8,128)S(1)}, bf16[4,100,720]{2,1,0:T(8,128)(2,1)}, f32[1,100,720]{2,1,0:T(8,128)S(1)}, /*index=5*/s32[]{:T(128)}, s32[]{:T(128)}) while((s32[]{:T(128)}, f32[1,100,720]{2,1,0:T(8,128)S(1)}, f32[1,100,720]{2,1,0:T(8,128)S(1)}, ...), condition=%wide.region_1.2_spmd.clone, body=%wide.region_0.1_spmd.clone.sunk | while | flops 720003 | bytes 1584099 | solution.py:90
  68.2 1.2 fusion.194
  69.4 1.2 fusion.194
  70.6 1.2 fusion.194
  71.7 1.2 fusion.194
  72.9 1.8 fusion.51
  74.8 1.7 fusion.49
  80.2 1.1 collective-permute-done.9
  81.2 2.4 collective-permute-done.8
  83.8 2.0 collective-permute-start.10
  85.8 0.9 fusion.54
  86.6 0.7 collective-permute-done.11
  91.1 0.7 convert_reduce_fusion
  94.2 0.9 copy-done.36
  95.2 40.8 %all-reduce = (f32[32,256]{1,0:T(8,128)S(1)}, f32[]{:T(128)}) all-reduce(f32[32,256]{1,0:T(8,128)S(1)} %broadcast_multiply_fusion, f32[]{:T(128)} %get-tuple-element.130), channel_id=1, replica_groups=mesh['member'=4,'lat'=4,'lon'=2] {'member','lat','lon'}, use_global_device_ids=true, to_apply=%region_9.10 | all-reduce | flops 8193 | bytes 65544 | tf_op jit(solution)/shard_map/psum | solution.py:148
  136.0 0.6 multiply_reduce_fusion.3
  137.9 0.6 broadcast_divide_fusion.3
  138.6 98.4 %all-reduce.4.cloned.1.call-done = (f32[9,100,256]{2,1,0:T(8,128)}, f32[9,256,256]{2,1,0:T(8,128)}, f32[100,256]{1,0:T(8,128)}) async-done(((f32[9,100,256]{2,1,0:T(8,128)}, f32[9,256,256]{2,1,0:T(8,128)}, f32[100,256]{1,0:T(8,128)}), (f32[9,100,256]{2,1,0:T(8,128)}, f32[9,256,256]{2,1,0:T(8,128)}, f32[100,256]{1,0:T(8,128)})) %all-reduce.4.cloned.1.call-update) | async-done | bytes 3383312 | tf_op jit(solution)/shard_map/psum | solution.py:148
  237.0 2.2 multiply_reduce_fusion.1
  239.9 2.2 broadcast_divide_fusion.1
  242.1 1.2 multiply_reduce_fusion
  244.0 1.6 broadcast_divide_fusion
  245.6 0.6 multiply_reduce_fusion.2
  247.0 0.7 broadcast_divide_fusion.2
  (165 shorter events, 16.6 us)
Async XLA Ops:
  7.2 43.9 %copy-start = (bf16[100,256]{1,0:T(8,128)(2,1)S(1)}, bf16[100,256]{1,0:T(8,128)(2,1)}, u32[]{:S(2)}) copy-start(bf16[100,256]{1,0:T(8,128)(2,1)} %param.16) | copy-start | bytes 153604
  7.2 229.8 %all-reduce.4.cloned.1.call-start = ((), (), s32[]{:S(2)}) async-start(), calls=%async_computation | async-start | bytes 6848512 | tf_op jit(solution)/shard_map/psum | solution.py:148
  8.5 6.8 %collective-permute-start.1 = (bf16[100,1,360]{2,1,0:T(2,128)(2,1)S(1)}, bf16[100,1,360]{2,1,0:T(2,128)(2,1)S(1)}, u32[]{:S(2)}, u32[]{:S(2)}) collective-permute-start(bf16[100,1,360]{2,1,0:T(2,128)(2,1)S(1)} %get-tuple-element.148), channel_id=1, source_target_pairs={{2,0},{4,2},{6,4},{0,6},{3,1},{5,3},{7,5},{1,7},{10,8},{12,10},{14... | collective-permute-start | bytes 216008 | tf_op jit(solution)/shard_map/ppermute | solution.py:18
  11.0 5.4 %collective-permute-start = (bf16[100,1,360]{2,1,0:T(2,128)(2,1)S(1)}, bf16[100,1,360]{2,1,0:T(2,128)(2,1)S(1)}, u32[]{:S(2)}, u32[]{:S(2)}) collective-permute-start(bf16[100,1,360]{2,1,0:T(2,128)(2,1)S(1)} %get-tuple-element.147), channel_id=1, source_target_pairs={{0,2},{2,4},{4,6},{6,0},{1,3},{3,5},{5,7},{7,1},{8,10},{10,12},{12... | collective-permute-start | bytes 216008 | tf_op jit(solution)/shard_map/ppermute | solution.py:15
  17.7 5.3 %collective-permute-start.3 = (bf16[100,4,1]{2,1,0:T(4,128)(2,1)S(1)}, bf16[100,4,1]{2,1,0:T(4,128)(2,1)S(1)}, u32[]{:S(2)}, u32[]{:S(2)}) collective-permute-start(bf16[100,4,1]{2,1,0:T(4,128)(2,1)S(1)} %get-tuple-element.133), channel_id=1, source_target_pairs={{1,0},{0,1},{3,2},{2,3},{5,4},{4,5},{7,6},{6,7},{9,8},{8,9},{11,10... | collective-permute-start | bytes 2408 | tf_op jit(solution)/shard_map/ppermute | solution.py:18
  19.2 4.8 %collective-permute-start.2 = (bf16[100,4,1]{2,1,0:T(4,128)(2,1)S(1)}, bf16[100,4,1]{2,1,0:T(4,128)(2,1)S(1)}, u32[]{:S(2)}, u32[]{:S(2)}) collective-permute-start(bf16[100,4,1]{2,1,0:T(4,128)(2,1)S(1)} %get-tuple-element.132), channel_id=1, source_target_pairs={{0,1},{1,0},{2,3},{3,2},{4,5},{5,4},{6,7},{7,6},{8,9},{9,8},{10,11... | collective-permute-start | bytes 2408 | tf_op jit(solution)/shard_map/ppermute | solution.py:15
  27.7 1.5 copy-start.40
  27.9 1.6 copy-start.33
  28.1 1.5 copy-start.31
  28.2 1.6 copy-start.29
  28.4 1.8 copy-start.27
  28.6 1.9 copy-start.25
  28.7 2.0 copy-start.23
  28.9 2.2 copy-start.21
  29.1 2.3 copy-start.19
  29.2 2.4 copy-start.37
  31.7 11.2 %copy-start.42 = (s32[2,360]{1,0:T(2,128)S(1)}, s32[2,360]{1,0:T(2,128)}, u32[]{:S(2)}) copy-start(s32[2,360]{1,0:T(2,128)} %param.12) | copy-start | bytes 8644
  31.7 11.2 %copy-start.2 = (bf16[100,2,360]{2,1,0:T(2,128)(2,1)S(1)}, bf16[100,2,360]{2,1,0:T(2,128)(2,1)}, u32[]{:S(2)}) copy-start(bf16[100,2,360]{2,1,0:T(2,128)(2,1)} %param.10) | copy-start | bytes 432004
  33.0 10.7 %copy-start.41 = (bf16[100,2,360]{2,1,0:T(2,128)(2,1)S(1)}, bf16[100,2,360]{2,1,0:T(2,128)(2,1)}, u32[]{:S(2)}) copy-start(bf16[100,2,360]{2,1,0:T(2,128)(2,1)} %param.11) | copy-start | bytes 432004
  33.0 5.4 %collective-permute-start.5 = (bf16[256,1,360]{0,2,1:T(8,128)(2,1)S(1)}, bf16[256,1,360]{0,2,1:T(8,128)(2,1)S(1)}, u32[]{:S(2)}, u32[]{:S(2)}) collective-permute-start(bf16[256,1,360]{0,2,1:T(8,128)(2,1)S(1)} %get-tuple-element.137), channel_id=1, source_target_pairs={{2,0},{4,2},{6,4},{0,6},{3,1},{5,3},{7,5},{1,7},{10,8},{12,10},{14... | collective-permute-start | bytes 552968 | tf_op jit(solution)/shard_map/ppermute | solution.py:18
  34.1 6.7 %collective-permute-start.4 = (bf16[256,1,360]{0,2,1:T(8,128)(2,1)S(1)}, bf16[256,1,360]{0,2,1:T(8,128)(2,1)S(1)}, u32[]{:S(2)}, u32[]{:S(2)}) collective-permute-start(bf16[256,1,360]{0,2,1:T(8,128)(2,1)S(1)} %get-tuple-element.136), channel_id=1, source_target_pairs={{0,2},{2,4},{4,6},{6,0},{1,3},{3,5},{5,7},{7,1},{8,10},{10,12},{12... | collective-permute-start | bytes 552968 | tf_op jit(solution)/shard_map/ppermute | solution.py:15
  40.8 3.9 %collective-permute-start.7 = (bf16[256,4,1]{0,2,1:T(2,128)(2,1)S(1)}, bf16[256,4,1]{0,2,1:T(2,128)(2,1)S(1)}, u32[]{:S(2)}, u32[]{:S(2)}) collective-permute-start(bf16[256,4,1]{0,2,1:T(2,128)(2,1)S(1)} %get-tuple-element.129), channel_id=1, source_target_pairs={{1,0},{0,1},{3,2},{2,3},{5,4},{4,5},{7,6},{6,7},{9,8},{8,9},{11,10... | collective-permute-start | bytes 6152 | tf_op jit(solution)/shard_map/ppermute | solution.py:18
  42.3 3.6 %collective-permute-start.6 = (bf16[256,4,1]{0,2,1:T(2,128)(2,1)S(1)}, bf16[256,4,1]{0,2,1:T(2,128)(2,1)S(1)}, u32[]{:S(2)}, u32[]{:S(2)}) collective-permute-start(bf16[256,4,1]{0,2,1:T(2,128)(2,1)S(1)} %get-tuple-element.128), channel_id=1, source_target_pairs={{0,1},{1,0},{2,3},{3,2},{4,5},{5,4},{6,7},{7,6},{8,9},{9,8},{10,11... | collective-permute-start | bytes 6152 | tf_op jit(solution)/shard_map/ppermute | solution.py:15
  46.3 1.3 copy-start.3
  46.7 1.4 copy-start.12
  46.7 1.4 copy-start.15
  46.7 1.4 copy-start.10
  46.7 1.7 copy-start.8
  46.8 1.9 copy-start.6
  46.8 2.2 copy-start.4
  46.8 3.0 %copy-start.17 = (bf16[256,2,360]{0,2,1:T(8,128)(2,1)}, bf16[256,2,360]{0,2,1:T(8,128)(2,1)S(1)}, u32[]{:S(2)}) copy-start(bf16[256,2,360]{0,2,1:T(8,128)(2,1)S(1)} %get-tuple-element.117) | copy-start | bytes 1105924
  49.8 1.4 copy-start.35
  74.8 1.8 copy-start.16
  76.5 1.3 copy-start.11
  76.8 1.3 copy-start.9
  76.9 1.6 copy-start.7
  76.9 4.4 %collective-permute-start.9 = (bf16[256,1,360]{0,2,1:T(8,128)(2,1)S(1)}, bf16[256,1,360]{0,2,1:T(8,128)(2,1)S(1)}, u32[]{:S(2)}, u32[]{:S(2)}) collective-permute-start(bf16[256,1,360]{0,2,1:T(8,128)(2,1)S(1)} %get-tuple-element.135), channel_id=1, source_target_pairs={{2,0},{4,2},{6,4},{0,6},{3,1},{5,3},{7,5},{1,7},{10,8},{12,10},{14... | collective-permute-start | bytes 552968 | tf_op jit(solution)/shard_map/ppermute | solution.py:18
  76.9 6.7 %collective-permute-start.8 = (bf16[256,1,360]{0,2,1:T(8,128)(2,1)S(1)}, bf16[256,1,360]{0,2,1:T(8,128)(2,1)S(1)}, u32[]{:S(2)}, u32[]{:S(2)}) collective-permute-start(bf16[256,1,360]{0,2,1:T(8,128)(2,1)S(1)} %get-tuple-element.134), channel_id=1, source_target_pairs={{0,2},{2,4},{4,6},{6,0},{1,3},{3,5},{5,7},{7,1},{8,10},{10,12},{12... | collective-permute-start | bytes 552968 | tf_op jit(solution)/shard_map/ppermute | solution.py:15
  80.1 7.2 %copy-start.14 = (f32[9,256,256]{2,1,0:T(8,128)}, f32[9,256,256]{2,1,0:T(8,128)S(1)}, u32[]{:S(2)}) copy-start(f32[9,256,256]{2,1,0:T(8,128)S(1)} %fusion.9) | copy-start | bytes 7077892
  83.7 3.7 %collective-permute-start.11 = (bf16[256,4,1]{0,2,1:T(2,128)(2,1)S(1)}, bf16[256,4,1]{0,2,1:T(2,128)(2,1)S(1)}, u32[]{:S(2)}, u32[]{:S(2)}) collective-permute-start(bf16[256,4,1]{0,2,1:T(2,128)(2,1)S(1)} %get-tuple-element.127), channel_id=1, source_target_pairs={{1,0},{0,1},{3,2},{2,3},{5,4},{4,5},{7,6},{6,7},{9,8},{8,9},{11,10... | collective-permute-start | bytes 6152 | tf_op jit(solution)/shard_map/ppermute | solution.py:18
  83.8 3.7 %collective-permute-start.10 = (bf16[256,4,1]{0,2,1:T(2,128)(2,1)S(1)}, bf16[256,4,1]{0,2,1:T(2,128)(2,1)S(1)}, u32[]{:S(2)}, u32[]{:S(2)}) collective-permute-start(bf16[256,4,1]{0,2,1:T(2,128)(2,1)S(1)} %get-tuple-element.126), channel_id=1, source_target_pairs={{0,1},{1,0},{2,3},{3,2},{4,5},{5,4},{6,7},{7,6},{8,9},{9,8},{10,11... | collective-permute-start | bytes 6152 | tf_op jit(solution)/shard_map/ppermute | solution.py:15
  91.1 1.4 copy-start.30
  91.8 1.2 copy-start.26
  92.0 1.2 copy-start.24
  92.3 1.2 copy-start.22
  92.5 1.2 copy-start.20
  237.0 5.1 %copy-start.1 = (f32[9,256,256]{2,1,0:T(8,128)S(1)}, f32[9,256,256]{2,1,0:T(8,128)}, u32[]{:S(2)}) copy-start(f32[9,256,256]{2,1,0:T(8,128)} %get-tuple-element.104) | copy-start | bytes 7077892
  244.0 1.6 copy-start.39
  (10 other events, 10.2 us)
Sparse Core Ops, SparseCore 0:
  95.2 141.7 all-reduce.3
where the time goes:
time: 256 us
  waiting for transfers between devices  119 us (46%)
  blocking collectives  57.6 us (22%)
  other arithmetic  20.7 us (8%)
  between operations  19.6 us (8%)
  matrix products  18.4 us (7%)
  starting transfers between devices  10.4 us (4%)
  local copies, waits for them, and re-layouts  9.45 us (4%)
    psum x1, waiting for transfers between devices, body(): lax.psum((grad_in, grad_mid, grad_out, grad_noise, loss_term), ('member',...  98.4 us
    psum x1, blocking collectives, body(): lax.psum((grad_in, grad_mid, grad_out, grad_noise, loss_term), ('member',...  40.8 us
    all_gather x1, blocking collectives, body(): lax.all_gather(output[None], 'member', axis=0, tiled=True)  16.8 us
    ppermute x6, waiting for transfers between devices, with_halo(): lax.ppermute(lax.slice_in_dim(block, 0, width, axis=dim), axis, backward)  12.8 us
    ppermute x6, waiting for transfers between devices, with_halo(): lax.ppermute(lax.slice_in_dim(block, block.shape[dim] - width, None, axis...  8.29 us
    dot_general x18, matrix products, conv_forward(): lax.dot_general(weights[offset], window, (((0,), (0,)), ((), ())), prefer...  6.96 us
    ppermute x6, starting transfers between devices, with_halo(): lax.ppermute(lax.slice_in_dim(block, 0, width, axis=dim), axis, backward)  6.79 us
  transfers between devices with their start and end apart: 13, of which 12 were waited for; matrix products, arithmetic and copies ran while one was open for 3% of the time, Pallas kernels for 0%

commit v1 on v0

--- a/solution.py
+++ b/solution.py
@@ -146,7 +146,7 @@
     grad_in = weight_grad(state_pad, delta_in, row_count, col_count)
     grad_noise = latent[:, None] * jnp.sum(delta_in.astype(jnp.float32), axis=1)[None, :]
     grad_in, grad_mid, grad_out, grad_noise, summed = lax.psum(
-        (grad_in, grad_mid, grad_out, grad_noise, loss_term), ("member", "lat", "lon")
+        lax.psum((grad_in, grad_mid, grad_out, grad_noise, loss_term), ("lat", "lon")), "member"
     )
     loss = summed / (variables * cell_count * lat_count * lax.axis_size("lon"))
     return (

time: 256 us -> 324 us (1.27)
  waiting for transfers between devices: 119 us -> 177 us
  blocking collectives: 57.6 us -> 66 us
    psum x1 -> x2, waiting for transfers between devices: 98.4 us -> 156 us  [the longest x1 81.9 us: body(): lax.psum(lax.psum((grad_in, grad_mid, grad_out, grad_noise, loss_term), (...]
    psum x1 -> x2, blocking collectives: 40.8 us -> 49.2 us  [the longest x1 26.7 us: body(): lax.psum((grad_in, grad_mid, grad_out, grad_noise, loss_term), ('lat', 'l...]
  transfers between devices with their start and end apart: 13 -> 14, of which waited for: 12 -> 13; matrix products, arithmetic and copies ran while one was open for 3% -> 2% of each run, Pallas kernels for 0% -> 0%
where the time goes in v1:
time: 324 us; the launch traced here: 323 us
  waiting for transfers between devices  177 us (55%)
  blocking collectives  66 us (20%)
  other arithmetic  20.7 us (6%)
  between operations  19.5 us (6%)
  matrix products  18.5 us (6%)
  local copies, waits for them, and re-layouts  10.9 us (3%)
  starting transfers between devices  10.4 us (3%)
    psum x1, waiting for transfers between devices, body(): lax.psum(lax.psum((grad_in, grad_mid, grad_out, grad_noise, loss_term), (...  81.9 us
    psum x1, waiting for transfers between devices, body(): lax.psum((grad_in, grad_mid, grad_out, grad_noise, loss_term), ('lat', 'l...  74.2 us
    psum x1, blocking collectives, body(): lax.psum((grad_in, grad_mid, grad_out, grad_noise, loss_term), ('lat', 'l...  26.7 us
    psum x1, blocking collectives, body(): lax.psum(lax.psum((grad_in, grad_mid, grad_out, grad_noise, loss_term), (...  22.6 us
    all_gather x1, blocking collectives, body(): lax.all_gather(output[None], 'member', axis=0, tiled=True)  16.7 us
    ppermute x6, waiting for transfers between devices, with_halo(): lax.ppermute(lax.slice_in_dim(block, 0, width, axis=dim), axis, backward)  12.7 us
    ppermute x6, waiting for transfers between devices, with_halo(): lax.ppermute(lax.slice_in_dim(block, block.shape[dim] - width, None, axis...  8.31 us
    dot_general x18, matrix products, conv_forward(): lax.dot_general(weights[offset], window, (((0,), (0,)), ((), ())), prefer...  6.98 us
  transfers between devices with their start and end apart: 14, of which 13 were waited for; matrix products, arithmetic and copies ran while one was open for 2% of the time, Pallas kernels for 0%

profile of v1, /device:TPU:0, one launch (start us, length us, event | category | flops | bytes accessed | tf_op | source)
XLA Modules:
  0.0 323.2 jit_solution(2839098449156446132)
XLA Ops:
  7.2 1.3 fusion.124
  8.5 2.5 collective-permute-start.1
  11.0 0.9 fusion.114
  11.9 3.4 %collective-permute-done.1 = bf16[100,1,360]{2,1,0:T(2,128)(2,1)S(1)} collective-permute-done((bf16[100,1,360]{2,1,0:T(2,128)(2,1)S(1)}, bf16[100,1,360]{2,1,0:T(2,128)(2,1)S(1)}, u32[]{:S(2)}, u32[]{:S(2)}) %collective-permute-start.1) | collective-permute-done | bytes 72032 | tf_op jit(solution)/shard_map/ppermute | solution.py:18
  15.3 1.1 collective-permute-done
  16.4 1.3 pad_maximum_fusion.2
  17.7 1.6 collective-permute-start.3
  19.8 3.2 collective-permute-done.3
  23.0 1.1 collective-permute-done.2
  24.1 2.2 maximum_select_fusion.2
  26.3 1.4 fusion.123
  31.7 1.3 multiply_convert_fusion
  33.0 1.0 collective-permute-start.5
  34.1 4.3 %collective-permute-done.5 = bf16[256,1,360]{0,2,1:T(8,128)(2,1)S(1)} collective-permute-done((bf16[256,1,360]{0,2,1:T(8,128)(2,1)S(1)}, bf16[256,1,360]{0,2,1:T(8,128)(2,1)S(1)}, u32[]{:S(2)}, u32[]{:S(2)}) %collective-permute-start.5) | collective-permute-done | bytes 184352 | tf_op jit(solution)/shard_map/ppermute | solution.py:18
  38.4 2.3 collective-permute-done.4
  40.8 1.6 collective-permute-start.7
  42.9 0.9 reshape.203
  43.8 0.9 reshape.204
  44.7 1.2 collective-permute-done.6
  46.8 0.8 copy-done.3
  49.8 1.3 add_convert_fusion
  51.1 0.8 copy-done.15
  52.2 16.7 %all-gather.1 = bf16[4,100,720]{2,1,0:T(8,128)(2,1)} all-gather(bf16[1,100,720]{2,1,0:T(8,128)(2,1)S(1)} %bitcast.306), channel_id=2, replica_groups=mesh['member'=4,'lat'=4,'lon'=2] {'member'}, dimensions={0}, use_global_device_ids=true | all-gather | bytes 720000 | tf_op jit(solution)/shard_map/all_gather | solution.py:128
  68.9 4.7 %while.15 = (s32[]{:T(128)}, f32[1,100,720]{2,1,0:T(8,128)S(1)}, f32[1,100,720]{2,1,0:T(8,128)S(1)}, bf16[4,100,720]{2,1,0:T(8,128)(2,1)}, f32[1,100,720]{2,1,0:T(8,128)S(1)}, /*index=5*/s32[]{:T(128)}, s32[]{:T(128)}) while((s32[]{:T(128)}, f32[1,100,720]{2,1,0:T(8,128)S(1)}, f32[1,100,720]{2,1,0:T(8,128)S(1)}, ...), condition=%wide.region_1.2_spmd.clone, body=%wide.region_0.1_spmd.clone.sunk | while | flops 720003 | bytes 1584099 | solution.py:90
  68.9 1.2 fusion.194
  70.1 1.2 fusion.194
  71.3 1.2 fusion.194
  72.5 1.2 fusion.194
  73.7 1.8 fusion.51
  75.5 1.7 fusion.49
  80.9 1.1 collective-permute-done.9
  82.0 2.5 collective-permute-done.8
  84.6 1.9 collective-permute-start.10
  86.5 0.9 fusion.54
  87.4 0.7 collective-permute-done.11
  91.9 0.7 convert_reduce_fusion
  94.9 0.9 copy-done.36
  95.9 74.2 %all-reduce.7.cloned.1.call-done = (f32[9,100,256]{2,1,0:T(8,128)}, f32[9,256,256]{2,1,0:T(8,128)}, f32[100,256]{1,0:T(8,128)}) async-done(((f32[9,100,256]{2,1,0:T(8,128)}, f32[9,256,256]{2,1,0:T(8,128)}, f32[100,256]{1,0:T(8,128)}), (f32[9,100,256]{2,1,0:T(8,128)}, f32[9,256,256]{2,1,0:T(8,128)}, f32[100,256]{1,0:T(8,128)})) %all-reduce.7.cloned.1.call-update) | async-done | bytes 3383312 | tf_op jit(solution)/shard_map/psum | solution.py:149
  170.2 0.6 copy-done.43
  170.9 26.7 %all-reduce = (f32[32,256]{1,0:T(8,128)S(1)}, f32[]{:T(128)}) all-reduce(f32[32,256]{1,0:T(8,128)S(1)} %broadcast_multiply_fusion, f32[]{:T(128)} %get-tuple-element.135), channel_id=1, replica_groups=mesh['member'=4,'lat'=4,'lon'=2] {'lat','lon'}, use_global_device_ids=true, to_apply=%region_12.13 | all-reduce | flops 8193 | bytes 65544 | tf_op jit(solution)/shard_map/psum | solution.py:149
  197.5 22.6 %all-reduce.2 = (f32[32,256]{1,0:T(8,128)S(1)}, f32[]{:T(128)}) all-reduce(f32[32,256]{1,0:T(8,128)S(1)} %get-tuple-element.101, f32[]{:T(128)} %get-tuple-element.102), channel_id=1, replica_groups=mesh['member'=4,'lat'=4,'lon'=2] {'member'}, use_global_device_ids=true, to_apply=%region_13.14 | all-reduce | flops 8193 | bytes 65544 | tf_op jit(solution)/shard_map/psum | solution.py:148
  222.7 81.9 %all-reduce.9.cloned.1.call-done = (f32[9,100,256]{2,1,0:T(8,128)}, f32[9,256,256]{2,1,0:T(8,128)}, f32[100,256]{1,0:T(8,128)}) async-done(((f32[9,100,256]{2,1,0:T(8,128)}, f32[9,256,256]{2,1,0:T(8,128)}, f32[100,256]{1,0:T(8,128)}), (f32[9,100,256]{2,1,0:T(8,128)}, f32[9,256,256]{2,1,0:T(8,128)}, f32[100,256]{1,0:T(8,128)})) %all-reduce.9.cloned.1.call-update) | async-done | bytes 3383312 | tf_op jit(solution)/shard_map/psum | solution.py:148
  304.6 2.2 multiply_reduce_fusion.1
  307.5 2.2 broadcast_divide_fusion.1
  309.7 1.2 multiply_reduce_fusion
  311.6 1.6 broadcast_divide_fusion
  313.2 0.6 multiply_reduce_fusion.2
  314.5 0.7 broadcast_divide_fusion.2
  (169 shorter events, 19.1 us)
Async XLA Ops:
  7.2 44.7 %copy-start = (bf16[100,256]{1,0:T(8,128)(2,1)S(1)}, bf16[100,256]{1,0:T(8,128)(2,1)}, u32[]{:S(2)}) copy-start(bf16[100,256]{1,0:T(8,128)(2,1)} %param.16) | copy-start | bytes 153604
  7.2 163.0 %all-reduce.7.cloned.1.call-start = ((), (), s32[]{:S(2)}) async-start(), calls=%async_computation | async-start | bytes 6848512 | tf_op jit(solution)/shard_map/psum | solution.py:149
  8.5 6.8 %collective-permute-start.1 = (bf16[100,1,360]{2,1,0:T(2,128)(2,1)S(1)}, bf16[100,1,360]{2,1,0:T(2,128)(2,1)S(1)}, u32[]{:S(2)}, u32[]{:S(2)}) collective-permute-start(bf16[100,1,360]{2,1,0:T(2,128)(2,1)S(1)} %get-tuple-element.153), channel_id=1, source_target_pairs={{2,0},{4,2},{6,4},{0,6},{3,1},{5,3},{7,5},{1,7},{10,8},{12,10},{14... | collective-permute-start | bytes 216008 | tf_op jit(solution)/shard_map/ppermute | solution.py:18
  11.0 5.4 %collective-permute-start = (bf16[100,1,360]{2,1,0:T(2,128)(2,1)S(1)}, bf16[100,1,360]{2,1,0:T(2,128)(2,1)S(1)}, u32[]{:S(2)}, u32[]{:S(2)}) collective-permute-start(bf16[100,1,360]{2,1,0:T(2,128)(2,1)S(1)} %get-tuple-element.152), channel_id=1, source_target_pairs={{0,2},{2,4},{4,6},{6,0},{1,3},{3,5},{5,7},{7,1},{8,10},{10,12},{12... | collective-permute-start | bytes 216008 | tf_op jit(solution)/shard_map/ppermute | solution.py:15
  17.7 5.3 %collective-permute-start.3 = (bf16[100,4,1]{2,1,0:T(4,128)(2,1)S(1)}, bf16[100,4,1]{2,1,0:T(4,128)(2,1)S(1)}, u32[]{:S(2)}, u32[]{:S(2)}) collective-permute-start(bf16[100,4,1]{2,1,0:T(4,128)(2,1)S(1)} %get-tuple-element.138), channel_id=1, source_target_pairs={{1,0},{0,1},{3,2},{2,3},{5,4},{4,5},{7,6},{6,7},{9,8},{8,9},{11,10... | collective-permute-start | bytes 2408 | tf_op jit(solution)/shard_map/ppermute | solution.py:18
  19.2 4.8 %collective-permute-start.2 = (bf16[100,4,1]{2,1,0:T(4,128)(2,1)S(1)}, bf16[100,4,1]{2,1,0:T(4,128)(2,1)S(1)}, u32[]{:S(2)}, u32[]{:S(2)}) collective-permute-start(bf16[100,4,1]{2,1,0:T(4,128)(2,1)S(1)} %get-tuple-element.137), channel_id=1, source_target_pairs={{0,1},{1,0},{2,3},{3,2},{4,5},{5,4},{6,7},{7,6},{8,9},{9,8},{10,11... | collective-permute-start | bytes 2408 | tf_op jit(solution)/shard_map/ppermute | solution.py:15
  27.7 1.5 copy-start.40
  27.9 1.7 copy-start.33
  28.1 1.5 copy-start.31
  28.2 1.6 copy-start.29
  28.4 1.8 copy-start.27
  28.6 1.9 copy-start.25
  28.7 2.0 copy-start.23
  28.9 2.2 copy-start.21
  29.2 2.4 copy-start.37
  31.7 11.2 %copy-start.42 = (s32[2,360]{1,0:T(2,128)S(1)}, s32[2,360]{1,0:T(2,128)}, u32[]{:S(2)}) copy-start(s32[2,360]{1,0:T(2,128)} %param.12) | copy-start | bytes 8644
  31.7 11.2 %copy-start.2 = (bf16[100,2,360]{2,1,0:T(2,128)(2,1)S(1)}, bf16[100,2,360]{2,1,0:T(2,128)(2,1)}, u32[]{:S(2)}) copy-start(bf16[100,2,360]{2,1,0:T(2,128)(2,1)} %param.10) | copy-start | bytes 432004
  33.0 10.7 %copy-start.41 = (bf16[100,2,360]{2,1,0:T(2,128)(2,1)S(1)}, bf16[100,2,360]{2,1,0:T(2,128)(2,1)}, u32[]{:S(2)}) copy-start(bf16[100,2,360]{2,1,0:T(2,128)(2,1)} %param.11) | copy-start | bytes 432004
  33.0 5.4 %collective-permute-start.5 = (bf16[256,1,360]{0,2,1:T(8,128)(2,1)S(1)}, bf16[256,1,360]{0,2,1:T(8,128)(2,1)S(1)}, u32[]{:S(2)}, u32[]{:S(2)}) collective-permute-start(bf16[256,1,360]{0,2,1:T(8,128)(2,1)S(1)} %get-tuple-element.142), channel_id=1, source_target_pairs={{2,0},{4,2},{6,4},{0,6},{3,1},{5,3},{7,5},{1,7},{10,8},{12,10},{14... | collective-permute-start | bytes 552968 | tf_op jit(solution)/shard_map/ppermute | solution.py:18
  34.1 6.7 %collective-permute-start.4 = (bf16[256,1,360]{0,2,1:T(8,128)(2,1)S(1)}, bf16[256,1,360]{0,2,1:T(8,128)(2,1)S(1)}, u32[]{:S(2)}, u32[]{:S(2)}) collective-permute-start(bf16[256,1,360]{0,2,1:T(8,128)(2,1)S(1)} %get-tuple-element.141), channel_id=1, source_target_pairs={{0,2},{2,4},{4,6},{6,0},{1,3},{3,5},{5,7},{7,1},{8,10},{10,12},{12... | collective-permute-start | bytes 552968 | tf_op jit(solution)/shard_map/ppermute | solution.py:15
  40.8 3.9 %collective-permute-start.7 = (bf16[256,4,1]{0,2,1:T(2,128)(2,1)S(1)}, bf16[256,4,1]{0,2,1:T(2,128)(2,1)S(1)}, u32[]{:S(2)}, u32[]{:S(2)}) collective-permute-start(bf16[256,4,1]{0,2,1:T(2,128)(2,1)S(1)} %get-tuple-element.134), channel_id=1, source_target_pairs={{1,0},{0,1},{3,2},{2,3},{5,4},{4,5},{7,6},{6,7},{9,8},{8,9},{11,10... | collective-permute-start | bytes 6152 | tf_op jit(solution)/shard_map/ppermute | solution.py:18
  42.3 3.6 %collective-permute-start.6 = (bf16[256,4,1]{0,2,1:T(2,128)(2,1)S(1)}, bf16[256,4,1]{0,2,1:T(2,128)(2,1)S(1)}, u32[]{:S(2)}, u32[]{:S(2)}) collective-permute-start(bf16[256,4,1]{0,2,1:T(2,128)(2,1)S(1)} %get-tuple-element.133), channel_id=1, source_target_pairs={{0,1},{1,0},{2,3},{3,2},{4,5},{5,4},{6,7},{7,6},{8,9},{9,8},{10,11... | collective-permute-start | bytes 6152 | tf_op jit(solution)/shard_map/ppermute | solution.py:15
  46.3 1.3 copy-start.3
  46.7 1.4 copy-start.12
  46.7 1.4 copy-start.17
  46.7 1.4 copy-start.10
  46.7 1.7 copy-start.8
  46.8 1.9 copy-start.6
  46.8 2.2 copy-start.4
  46.8 3.0 copy-start.19
  49.8 2.1 copy-start.35
  75.5 1.8 copy-start.18
  77.3 1.3 copy-start.11
  77.6 1.3 copy-start.9
  77.6 1.6 copy-start.7
  77.6 4.3 %collective-permute-start.9 = (bf16[256,1,360]{0,2,1:T(8,128)(2,1)S(1)}, bf16[256,1,360]{0,2,1:T(8,128)(2,1)S(1)}, u32[]{:S(2)}, u32[]{:S(2)}) collective-permute-start(bf16[256,1,360]{0,2,1:T(8,128)(2,1)S(1)} %get-tuple-element.140), channel_id=1, source_target_pairs={{2,0},{4,2},{6,4},{0,6},{3,1},{5,3},{7,5},{1,7},{10,8},{12,10},{14... | collective-permute-start | bytes 552968 | tf_op jit(solution)/shard_map/ppermute | solution.py:18
  77.7 6.7 %collective-permute-start.8 = (bf16[256,1,360]{0,2,1:T(8,128)(2,1)S(1)}, bf16[256,1,360]{0,2,1:T(8,128)(2,1)S(1)}, u32[]{:S(2)}, u32[]{:S(2)}) collective-permute-start(bf16[256,1,360]{0,2,1:T(8,128)(2,1)S(1)} %get-tuple-element.139), channel_id=1, source_target_pairs={{0,2},{2,4},{4,6},{6,0},{1,3},{3,5},{5,7},{7,1},{8,10},{10,12},{12... | collective-permute-start | bytes 552968 | tf_op jit(solution)/shard_map/ppermute | solution.py:15
  80.2 6.3 %copy-start.16 = (bf16[256,720]{0,1:T(8,128)(2,1)S(1)}, bf16[256,720]{0,1:T(8,128)(2,1)}, u32[]{:S(2)}) copy-start(bf16[256,720]{0,1:T(8,128)(2,1)} %copy-done.15) | copy-start | bytes 1105924
  80.9 7.2 %copy-start.14 = (f32[9,256,256]{2,1,0:T(8,128)}, f32[9,256,256]{2,1,0:T(8,128)S(1)}, u32[]{:S(2)}) copy-start(f32[9,256,256]{2,1,0:T(8,128)S(1)} %fusion.9) | copy-start | bytes 7077892
  84.4 3.7 %collective-permute-start.11 = (bf16[256,4,1]{0,2,1:T(2,128)(2,1)S(1)}, bf16[256,4,1]{0,2,1:T(2,128)(2,1)S(1)}, u32[]{:S(2)}, u32[]{:S(2)}) collective-permute-start(bf16[256,4,1]{0,2,1:T(2,128)(2,1)S(1)} %get-tuple-element.132), channel_id=1, source_target_pairs={{1,0},{0,1},{3,2},{2,3},{5,4},{4,5},{7,6},{6,7},{9,8},{8,9},{11,10... | collective-permute-start | bytes 6152 | tf_op jit(solution)/shard_map/ppermute | solution.py:18
  84.6 3.6 %collective-permute-start.10 = (bf16[256,4,1]{0,2,1:T(2,128)(2,1)S(1)}, bf16[256,4,1]{0,2,1:T(2,128)(2,1)S(1)}, u32[]{:S(2)}, u32[]{:S(2)}) collective-permute-start(bf16[256,4,1]{0,2,1:T(2,128)(2,1)S(1)} %get-tuple-element.131), channel_id=1, source_target_pairs={{0,1},{1,0},{2,3},{3,2},{4,5},{5,4},{6,7},{7,6},{8,9},{9,8},{10,11... | collective-permute-start | bytes 6152 | tf_op jit(solution)/shard_map/ppermute | solution.py:15
  91.9 1.4 copy-start.30
  92.6 1.2 copy-start.26
  92.8 1.2 copy-start.24
  93.0 1.2 copy-start.22
  95.9 208.7 %all-reduce.9.cloned.1.call-start = ((), (), s32[]{:S(2)}) async-start(), calls=%async_computation.1 | async-start | bytes 6848512 | tf_op jit(solution)/shard_map/psum | solution.py:148
  304.6 5.1 %copy-start.1 = (f32[9,256,256]{2,1,0:T(8,128)S(1)}, f32[9,256,256]{2,1,0:T(8,128)}, u32[]{:S(2)}) copy-start(f32[9,256,256]{2,1,0:T(8,128)} %get-tuple-element.109) | copy-start | bytes 7077892
  311.6 1.6 copy-start.39
  (11 other events, 10.6 us)
Sparse Core Ops, SparseCore 0:
  96.0 74.0 all-reduce.6
  172.7 131.8 all-reduce.8
